TPU v7x, 256 devices: a whole 4x4x8 slice. The times are simulated.
256 devices in a mesh: rep: 4 (over x), fsdp: 32 (over z_lo, y, core), tp: 2 (over z_hi).
Axes of the slice: x: 4, y: 4, z: 8 (z_hi: 2, z_lo: 4; z = z_hi * 4 + z_lo), core: 2. Of those that a mesh axis runs over, the one named last changes fastest.
Arguments:
- hidden: bfloat16 [32768, 4096], P(('rep', 'fsdp')), may hold values from -24 to 24
- norm_gain: float32 [4096], P('fsdp'), may hold values from 0.5 to 1.5
- value_weight: bfloat16 [4096, 1024], P('fsdp', 'tp'), may hold values from -0.09375 to 0.09375
- value_grad: bfloat16 [32768, 1024], P(('rep', 'fsdp'), 'tp'), may hold values from -6 to 6
Outputs:
- input_grad: bfloat16 [32768, 4096], P(('rep', 'fsdp'))
- weight_grad: float32 [4096, 1024], P('fsdp', 'tp')
- gain_grad: float32 [4096], P('fsdp')
All inputs are finite; a program needn't handle non-finite values.
Results may differ from a plain program's by a relative error of at most 0.00125.
Values may be sent and summed in bfloat16 or wider, within the bound.
A program may use at most 64 MiB of HBM per device.

v0:
```python
import jax
import jax.numpy as jnp
from jax import lax
from jax.sharding import PartitionSpec as P

epsilon = 1e-05


def gathered_total(array, axis):
    return lax.all_gather(array, axis).sum(0)


def local(hidden, norm_gain, value_weight, value_grad):
    average = 1.0 / (lax.axis_size("rep") * lax.axis_size("fsdp"))
    inputs = hidden.astype(jnp.float32)
    inv_local = lax.rsqrt(jnp.mean(inputs * inputs, axis=1, keepdims=True) + epsilon)
    full_gain = lax.all_gather(norm_gain, "fsdp", axis=0, tiled=True)
    normal = inputs * inv_local
    normed = (normal * full_gain).astype(jnp.bfloat16)

    def project(weight_piece):
        return jnp.dot(value_grad, weight_piece.T, preferred_element_type=jnp.float32)

    partial_grad = project(lax.all_gather(value_weight, "fsdp", axis=0, tiled=True))
    grad_normed = gathered_total(partial_grad, "tp")

    def weight_term(number_rows):
        feature_block = lax.slice_in_dim(normed, 0, number_rows, axis=1)
        return jnp.dot(feature_block.T, value_grad, preferred_element_type=jnp.float32)

    weight_part = lax.psum_scatter(
        weight_term(value_weight.shape[0] * lax.axis_size("fsdp")),
        "fsdp",
        scatter_dimension=0,
        tiled=True,
    )
    gain_part = lax.psum_scatter(
        jnp.sum(grad_normed * normal, axis=0), "fsdp", scatter_dimension=0, tiled=True
    )
    grad_scaled = grad_normed * full_gain
    center = jnp.mean(grad_scaled * normal, axis=1, keepdims=True)
    input_grad = (inv_local * (grad_scaled - normal * center)).astype(jnp.bfloat16)
    weight_total = gathered_total(weight_part, "rep")
    gain_total = gathered_total(gain_part, "rep")
    return (input_grad, weight_total * average, gain_total * average)


def solution(mesh):
    return jax.shard_map(
        local,
        mesh=mesh,
        in_specs=(P(("rep", "fsdp"), None), P("fsdp"), P("fsdp", "tp"), P(("rep", "fsdp"), "tp")),
        out_specs=(P(("rep", "fsdp"), None), P("fsdp", "tp"), P("fsdp")),
        check_vma=False,
    )
```

profile of v0, /device:TPU:24, one launch (start us, length us, event | category | flops | bytes accessed | tf_op | source)
XLA Modules:
  0.0 474.5 jit_solution(6921891645463938345)
XLA Ops:
  7.2 0.7 all-gather.9.cloned.1.call-update
  7.9 0.0 all-gather.11.cloned.1.call-start
  8.0 66.3 %all-gather.9.cloned.1.call-done = bf16[4096,512]{1,0:T(8,128)(2,1)} async-done(((bf16[128,512]{1,0:T(8,128)(2,1)}), bf16[4096,512]{1,0:T(8,128)(2,1)}) %all-gather.9.cloned.1.call-update) | async-done | bytes 4194320 | tf_op jit(solution)/shard_map/all_gather | solution.py:24
  74.2 5.4 %fusion.15 = f32[256,4096]{1,0:T(8,128)} fusion(bf16[256,512]{1,0:T(8,128)(2,1)S(1)} %copy-done, bf16[4096,512]{1,0:T(8,128)(2,1)} %all-gather.9.cloned.1.call-done), kind=kOutput, calls=%fused_computation.21 | convolution fusion | flops 1073741824 | bytes 8650752 | tf_op jit(solution)/shard_map/dot_general | solution.py:22
  79.7 0.0 reduce-scatter.2.cloned.1.call-start
  79.7 0.6 copy-done.2
  80.3 34.4 %all-gather.3 = f32[32,1,128]{2,1,0:T(1,128)S(1)} all-gather(f32[1,1,128]{2,1,0:T(1,128)S(1)} %bitcast.15), channel_id=1, replica_groups=mesh['rep'=4,'fsdp'=32,'tp'=2] {'fsdp'}, dimensions={0}, use_global_device_ids=true | all-gather | bytes 16896 | tf_op jit(solution)/shard_map/all_gather | solution.py:17
  114.7 0.5 fusion.10
  115.2 4.6 fusion.11
  119.9 0.0 all-gather.13.cloned.1.call-start
  119.9 0.6 copy-done.3
  120.5 0.6 dynamic-slice
  121.8 161.8 %all-gather.11.cloned.1.call-done = f32[512,4096]{1,0:T(8,128)} async-done(((f32[256,4096]{1,0:T(8,128)}), f32[512,4096]{1,0:T(8,128)}) %all-gather.11.cloned.1.call-update) | async-done | bytes 8388624 | tf_op jit(solution)/shard_map/all_gather | solution.py:10
  283.6 6.4 %reduce_sum.55 = f32[256,4096]{1,0:T(8,128)} reduce(f32[2,256,4096]{2,1,0:T(8,128)} %bitcast.10, f32[]{:T(128)} %constant.4.clone.1), dimensions={0}, to_apply=%region_1.0 | reduce | flops 1048576 | bytes 12582916 | tf_op jit(solution)/shard_map/reduce_sum | solution.py:10
  289.9 3.4 fusion.9
  293.4 118.5 %all-reduce = f32[4096]{0:T(1024)S(1)} all-reduce(f32[4096]{0:T(1024)S(1)} %get-tuple-element.3), channel_id=6, replica_groups=mesh['rep'=4,'fsdp'=32,'tp'=2] {'fsdp'}, use_global_device_ids=true, to_apply=%region_6.0.clone | all-reduce | flops 4096 | bytes 32768
  411.8 11.6 %reduce-scatter.2.cloned.1.call-done = f32[128,512]{1,0:T(8,128)} async-done(((f32[4096,512]{1,0:T(8,128)}), f32[128,512]{1,0:T(8,128)}) %reduce-scatter.2.cloned.1.call-update) | async-done | bytes 262160 | tf_op jit(solution)/shard_map/reduce_scatter | solution.py:31
  423.5 0.1 dynamic-slice_bitcast_fusion
  423.6 10.0 %all-gather.4 = f32[4,1,128]{2,1,0:T(1,128)S(1)} all-gather(f32[1,1,128]{2,1,0:T(1,128)S(1)} %dynamic-slice_bitcast_fusion), channel_id=4, replica_groups=mesh['rep'=4,'fsdp'=32,'tp'=2] {'rep'}, dimensions={0}, use_global_device_ids=true | all-gather | bytes 2560 | tf_op jit(solution)/shard_map/all_gather | solution.py:10
  433.6 0.5 broadcast_multiply_fusion.2
  434.1 4.7 fusion.7
  438.8 27.1 %all-gather.13.cloned.1.call-done = f32[512,512]{1,0:T(8,128)} async-done(((f32[128,512]{1,0:T(8,128)}), f32[512,512]{1,0:T(8,128)}) %all-gather.13.cloned.1.call-update) | async-done | bytes 1048592 | tf_op jit(solution)/shard_map/all_gather | solution.py:10
  465.9 1.3 reduce_sum.57
  467.2 0.7 broadcast_multiply_fusion
  (13 shorter events, 0.1 us)
Async XLA Ops:
  7.2 67.1 %copy-start = (bf16[256,512]{1,0:T(8,128)(2,1)S(1)}, bf16[256,512]{1,0:T(8,128)(2,1)}, u32[]{:S(2)}) copy-start(bf16[256,512]{1,0:T(8,128)(2,1)} %param.7) | copy-start | bytes 786436
  7.2 67.1 %all-gather.9.cloned.1.call-start = ((), (), s32[]{:S(2)}) async-start(), calls=%async_computation.1 | async-start | bytes 4325376 | tf_op jit(solution)/shard_map/all_gather | solution.py:24
  7.9 275.7 %all-gather.11.cloned.1.call-start = ((), (), s32[]{:S(2)}) async-start(), calls=%async_computation.3 | async-start | bytes 12582912 | tf_op jit(solution)/shard_map/all_gather | solution.py:10
  79.6 0.7 copy-start.2
  79.6 35.1 %copy-start.1 = (bf16[256,4096]{1,0:T(8,128)(2,1)S(1)}, bf16[256,4096]{1,0:T(8,128)(2,1)}, u32[]{:S(2)}) copy-start(bf16[256,4096]{1,0:T(8,128)(2,1)} %param.4) | copy-start | bytes 6291460
  79.7 343.8 %reduce-scatter.2.cloned.1.call-start = ((), (), s32[]{:S(2)}) async-start(), calls=%async_computation.2 | async-start | bytes 8650752 | tf_op jit(solution)/shard_map/reduce_scatter | solution.py:31
  119.8 0.7 copy-start.3
  119.9 346.0 %all-gather.13.cloned.1.call-start = ((), (), s32[]{:S(2)}) async-start(), calls=%async_computation.4 | async-start | bytes 1310720 | tf_op jit(solution)/shard_map/all_gather | solution.py:10
Sparse Core Ops, SparseCore 0:
  9.8 64.3 all-gather.8
  79.8 203.7 all-gather.10
  286.1 137.3 reduce-scatter.1
  425.1 40.6 all-gather.12
where the time goes:
time: 475 us; the launch traced here: 474 us
  waiting for transfers between devices  268 us (56%)
  blocking collectives  163 us (34%)
  other arithmetic  17.6 us (4%)
  between operations  14.4 us (3%)
  matrix products  10 us (2%)
    all_gather x2, waiting for transfers between devices, gathered_total(): return lax.all_gather(array, axis).sum(0)  189 us
    unnamed x1, blocking collectives  118 us
    all_gather x1, waiting for transfers between devices, local(): lax.all_gather(value_weight, 'fsdp', axis=0, tiled=True)  66.3 us
    all_gather x1, blocking collectives, local(): full_gain = lax.all_gather(norm_gain, 'fsdp', axis=0, tiled=True)  34.4 us
    reduce_scatter x1, waiting for transfers between devices, local(): lax.psum_scatter(weight_term(value_weight.shape[0] * lax.axis_size('fsdp'...  11.6 us
    all_gather x1, blocking collectives, gathered_total(): return lax.all_gather(array, axis).sum(0)  9.96 us
  transfers between devices with their start and end apart: 4, of which 4 were waited for; matrix products, arithmetic and copies ran while one was open for 4% of the time, Pallas kernels for 0%

commit v1 on v0

v1 whole, which is shorter than its diff:
```python
import jax
import jax.numpy as jnp
from jax import lax
from jax.experimental import pallas as pl
from jax.experimental.pallas import tpu as pltpu
from jax.sharding import PartitionSpec as P

EPS = 1e-05
D = 4096
F32 = jnp.float32
BF16 = jnp.bfloat16
MESH = pl.DeviceIdType.MESH


def kernel(hidden, gain_in, weight_in, grad_in, out_x, out_w, out_g, s):
    rep, fs, tp = lax.axis_index("rep"), lax.axis_index("fsdp"), lax.axis_index("tp")
    X, C, Y = rep, fs % 2, (fs // 2) % 4
    zl, zh = fs // 8, tp
    Z = zh * 4 + zl
    average = 1.0 / 128.0

    def dev(x, y, z, c):
        x, y, z, c = x % 4, y % 4, z % 8, c % 2
        return (x, ((z % 4) * 4 + y) * 2 + c, z // 4)

    def zpeer(k):
        return zh * 4 + (zl + k) % 4

    sibling = dev(X, Y, Z, C + 1)
    started = []

    def send(src, dst, sems, index, target):
        copy = pltpu.make_async_remote_copy(
            src_ref=src,
            dst_ref=dst,
            send_sem=s["sent"].at[len(started)],
            recv_sem=sems.at[index],
            device_id=target,
            device_id_type=MESH,
        )
        copy.start()
        started.append(copy)

    def arrived(dst, sems, index):
        pltpu.make_async_remote_copy(
            src_ref=dst,
            dst_ref=dst,
            send_sem=s["sent"].at[0],
            recv_sem=sems.at[index],
            device_id=sibling,
            device_id_type=MESH,
        ).wait_recv()

    me = X * 2 + C
    wbuf, vgx, vga, hid, hx = s["wbuf"], s["vgx"], s["vga"], s["hid"], s["hx"]
    gainb, invt, invx = s["gainb"], s["invt"], s["invx"]

    w_own = pltpu.make_async_copy(weight_in, wbuf.at[C, Z, Y], s["l_w"])
    w_own.start()
    vg_own = pltpu.make_async_copy(grad_in, vgx.at[me], s["l_vg"].at[0])
    vg_own.start()
    vg_own2 = pltpu.make_async_copy(grad_in, vga.at[zh], s["l_vg"].at[1])
    vg_own2.start()
    loads = []
    for b in range(32):
        load = pltpu.make_async_copy(hidden.at[:, b * 128 : (b + 1) * 128], hid.at[b], s["l_h"].at[b])
        load.start()
        loads.append(load)
    gainb[C, zl, Y] = jnp.broadcast_to(gain_in[...], (8, 128))

    barrier = pltpu.get_barrier_semaphore()

    def greet(target):
        pl.semaphore_signal(barrier, inc=1, device_id=target, device_id_type=MESH)

    for k in range(1, 4):
        for c in range(2):
            greet(dev(X + k, Y, Z, c))
        greet(dev(X, Y + k, Z, C))
        greet(dev(X, Y, zpeer(k), C))
        greet(dev(Y, Y + k, Z, C))
    greet(sibling)
    greet(dev(X, Y, Z + 1, C))
    greet(dev(X, Y, Z - 1, C))
    greet(dev(X, Y, Z + 4, C))

    @pl.when(X != Y)
    def _():
        greet(dev(Y, Y, Z, C))

    pl.semaphore_wait(barrier, 19 + jnp.where(X != Y, 1, 0))

    w_own.wait()

    def w_a(c, z):
        return wbuf.at[c, z, :, 0]

    def w_b(c, z):
        return wbuf.at[c, z, :, 1]

    def w_b1(z, y):
        return wbuf.at[C, z, y, 1]

    for k in (1, 3, 2):
        send(wbuf.at[C, Z, Y, 0], wbuf.at[C, Z, Y, 0], s["a_y"], k, dev(X, Y + k, Z, C))
    send(w_b1(Z, Y), w_b1(Z, Y), s["b_p"], 1, dev(X, Y, Z + 1, C))
    send(w_b1(Z, Y), w_b1(Z, Y), s["b_m"], 1, dev(X, Y, Z - 1, C))
    for k in (1, 3, 2):
        send(gainb.at[C, zl, Y], gainb.at[C, zl, Y], s["g_y"], k, dev(X, Y + k, Z, C))
    vg_own.wait()
    vg_own2.wait()
    for k in (1, 3, 2):
        send(vgx.at[me], vgx.at[me], s["vg_x"], k, dev(X + k, Y, Z, C))
    send(vgx.at[me], vgx.at[me], s["vg_c"], 0, sibling)
    send(vga.at[zh], vga.at[zh], s["vg_t"], 0, dev(X, Y, Z + 4, C))

    def b_to_y(z):
        for k in (1, 3, 2):
            send(w_b1(z, Y), w_b1(z, Y), s["b_y"], (z, k), dev(X, Y + k, Z, C))

    b_to_y(Z)

    for load in loads:
        load.wait()
    own = []
    for zp in range(4):
        for k in (1, 3, 2):
            x = (X + k) % 4
            for c in range(2):
                send(hid.at[zp * 8 + x * 2 + c], hx.at[zp, me], s["h_x"], (zp, me), dev(X + k, Y, Z, c))
        send(hid.at[zp * 8 + X * 2 + 1 - C], hx.at[zp, me], s["h_x"], (zp, me), sibling)
        copy = pltpu.make_async_copy(hid.at[zp * 8 + me], hx.at[zp, me], s["l_o"].at[zp])
        copy.start()
        own.append(copy)

    def square(b, total):
        value = hid[b].astype(F32)
        return total + value * value

    squares = lax.fori_loop(0, 32, square, jnp.zeros((256, 128), F32))
    inv = lax.rsqrt(jnp.sum(squares, axis=1, keepdims=True) * (1.0 / D) + EPS)
    invb = jnp.broadcast_to(inv, (256, 128))
    s["invb"][...] = invb
    invt[...] = jnp.transpose(invb)[:8]
    for k in (1, 3, 2):
        for c in range(2):
            send(invt, invx.at[me], s["i_x"], me, dev(X + k, Y, Z, c))
    send(invt, invx.at[me], s["i_x"], me, sibling)
    s["invc"][me] = invb

    def a_step(k):
        p, m = (Z - k) % 8, (Z + k) % 8
        if k == 0:
            for j in (1, 3, 2):
                arrived(wbuf.at[C, Z, Y - j + jnp.where(Y < j, 4, 0), 0], s["a_y"], j)
            send(w_a(C, Z), w_a(C, Z), s["a_p"], 1, dev(X, Y, Z + 1, C))
            send(w_a(C, Z), w_a(C, Z), s["a_m"], 1, dev(X, Y, Z - 1, C))
            send(w_a(C, Z), w_a(C, Z), s["d_a"], Z, sibling)
        elif k < 4:
            for z, sems, step, part in ((p, s["a_p"], 1, 0), (m, s["a_m"], -1, 2)):
                arrived(w_a(C, z), sems, k)
                if k < 3:
                    send(w_a(C, z), w_a(C, z), sems, k + 1, dev(X, Y, Z + step, C))
                else:
                    half = wbuf.at[C, z, part : part + 2, 0]
                    send(half, half, sems, 4, dev(X, Y, Z + step, C))
                send(w_a(C, z), w_a(C, z), s["d_a"], z, sibling)
        else:
            arrived(wbuf.at[C, p, 0:2, 0], s["a_p"], 4)
            arrived(wbuf.at[C, p, 2:4, 0], s["a_m"], 4)
            send(w_a(C, p), w_a(C, p), s["d_a"], p, sibling)

    def b_step(k):
        p, m = (Z - k) % 8, (Z + k) % 8
        if k < 4:
            for z, sems, step, part in ((p, s["b_p"], 1, 0), (m, s["b_m"], -1, 32)):
                arrived(w_b1(z, Y), sems, k)
                if k < 3:
                    send(w_b1(z, Y), w_b1(z, Y), sems, k + 1, dev(X, Y, Z + step, C))
                else:
                    half = wbuf.at[C, z, Y, 1, part : part + 32]
                    send(half, half, sems, 4, dev(X, Y, Z + step, C))
                b_to_y(z)
        else:
            arrived(wbuf.at[C, p, Y, 1, 0:32], s["b_p"], 4)
            arrived(wbuf.at[C, p, Y, 1, 32:64], s["b_m"], 4)
            b_to_y(p)

    def b_core(z):
        for j in (1, 3, 2):
            arrived(w_b1(z, (Y - j) % 4), s["b_y"], (z, j))
        send(w_b(C, z), w_b(C, z), s["d_b"], z, sibling)

    a_step(0)
    b_step(1)

    for j in (1, 3, 2):
        arrived(gainb.at[C, zl, (Y - j) % 4], s["g_y"], j)
    for k in range(1, 4):
        send(gainb.at[C, zl], gainb.at[C, zl], s["g_z"], k, dev(X, Y, zpeer(k), C))

    a_step(1)
    b_core(Z)
    b_step(2)
    for j in (1, 3, 2):
        x = ((X - j) % 4) * 2 + C
        arrived(vgx.at[x], s["vg_x"], j)
        send(vgx.at[x], vgx.at[x], s["vg_c"], j, sibling)
    for j in range(1, 4):
        arrived(gainb.at[C, (zl - j) % 4], s["g_z"], j)
    send(gainb.at[C], gainb.at[C], s["g_c"], 0, sibling)

    a_step(2)
    b_core((Z - 1) % 8)
    b_core((Z + 1) % 8)
    b_step(3)

    for k in range(1, 8):
        src = (me + k) % 8
        arrived(invx.at[src], s["i_x"], src)
        row = jnp.broadcast_to(invx[src, 0:1], (128, 256))
        s["invc"][src] = jnp.transpose(row)
    for j in range(4):
        src = ((X - j) % 4) * 2 + 1 - C
        arrived(vgx.at[src], s["vg_c"], j)
    arrived(gainb.at[1 - C], s["g_c"], 0)

    part, yrecv, zrecv, ysum = s["part"], s["yrecv"], s["zrecv"], s["ysum"]

    def weight_chunk(zp):
        own[zp].wait()
        for k in range(1, 8):
            src = (me + k) % 8
            arrived(hx.at[zp, src], s["h_x"], (zp, src))
        gain = gainb[C, zp, X]

        def scale(src, _):
            value = (hx[zp, src].astype(F32) * s["invc"][src]).reshape(32, 8, 128) * gain[None]
            s["normed"][src] = value.reshape(256, 128).astype(BF16)
            return 0

        lax.fori_loop(0, 8, scale, 0)
        product = lax.dot_general(
            s["normed"][...].reshape(2048, 128),
            vgx[...].reshape(2048, 512),
            (((0,), (0,)), ((), ())),
            preferred_element_type=F32,
        )
        part[zp] = product.reshape(4, 32, 512)
        for k in (1, 3, 2):
            send(part.at[zp, (Y + k) % 4], yrecv.at[zp, Y], s["r_y"], (zp, Y), dev(X, Y + k, Z, C))

    gg = s["gg"]

    def input_chunk(zq):
        for h in range(2):
            arrived(w_a(1 - C, zq + 4 * h), s["d_a"], zq + 4 * h)
            arrived(w_b(1 - C, zq + 4 * h), s["d_b"], zq + 4 * h)

        def core(c, _):
            product = None
            for h in range(2):
                term = lax.dot_general(
                    vga[h],
                    wbuf[c, zq + 4 * h].reshape(512, 512),
                    (((1,), (1,)), ((), ())),
                    preferred_element_type=F32,
                )
                product = term if product is None else product + term
            for y in range(4):
                value = product[:, y * 128 : (y + 1) * 128]
                b = zq * 8 + y * 2 + c
                share = value * (hid[b].astype(F32) * s["invb"][...])
                share = share.reshape(32, 8, 128)
                gg[c, y, zq] = jnp.sum(share, axis=0)
                gain = gainb[c, zq, y][None]
                s["center"][...] += (share * gain).reshape(256, 128)
                s["gs"][b] = (value.reshape(32, 8, 128) * gain).reshape(256, 128)
            return 0

        lax.fori_loop(0, 2, core, 0)

    s["center"][...] = jnp.zeros((256, 128), F32)

    weight_chunk(0)
    a_step(3)
    b_core((Z - 2) % 8)
    b_core((Z + 2) % 8)
    b_step(4)
    weight_chunk(1)
    a_step(4)
    arrived(vga.at[1 - zh], s["vg_t"], 0)
    input_chunk((zl + 2) % 4)
    weight_chunk(2)
    b_core((Z - 3) % 8)
    b_core((Z + 3) % 8)
    input_chunk((zl + 1) % 4)
    input_chunk((zl + 3) % 4)
    weight_chunk(3)
    b_core((Z + 4) % 8)

    def y_total(zp):
        total = part[zp, Y]
        for j in range(1, 4):
            src = (Y + j) % 4
            arrived(yrecv.at[zp, src], s["r_y"], (zp, src))
            total = total + yrecv[zp, src]
        ysum[zp] = total

    for zp in range(4):
        y_total(zp)
    for k in range(1, 4):
        send(ysum.at[(zl + k) % 4], zrecv.at[zl], s["r_z"], zl, dev(X, Y, zpeer(k), C))

    input_chunk(zl)

    g1, g2, g3, gr1, gr2, gr3, gr4 = (s[n] for n in ("g1", "g2", "g3", "gr1", "gr2", "gr3", "gr4"))
    send(gg.at[1 - C], gr1, s["q_c"], 0, sibling)

    total = ysum[zl]
    for j in range(1, 4):
        src = (zl + j) % 4
        arrived(zrecv.at[src], s["r_z"], src)
        total = total + zrecv[src]
    s["fin"][...] = total * average
    dlv = s["dlv"]
    for k in range(1, 4):
        send(s["fin"], dlv.at[Y], s["r_d"], Y, dev(X + k, X, Z, C))

    @pl.when(X == Y)
    def _():
        dlv[Y] = s["fin"][...]

    def to_diagonal():
        return pltpu.make_async_remote_copy(
            src_ref=s["fin"],
            dst_ref=dlv.at[Y],
            send_sem=s["r_s"],
            recv_sem=s["r_d"].at[Y],
            device_id=dev(X, X, Z, C),
            device_id_type=MESH,
        )

    @pl.when(X != Y)
    def _():
        to_diagonal().start()

    arrived(gr1, s["q_c"], 0)
    g1[...] = gg[C] + gr1[...]
    for k in (1, 3, 2):
        send(g1.at[(Y + k) % 4], gr2.at[Y], s["q_y"], Y, dev(X, Y + k, Z, C))

    center = jnp.sum(s["center"][...], axis=1, keepdims=True) * (1.0 / D)
    s["center"][...] = jnp.broadcast_to(center, (256, 128)) * s["invb"][...]

    def finish(b):
        normal_center = hid[b].astype(F32) * s["center"][...]
        out_x[:, b * 128 : (b + 1) * 128] = (s["invb"][...] * (s["gs"][b] - normal_center)).astype(BF16)

    for b in range(16):
        finish(b)
    gr2[Y] = g1[Y]
    for j in range(1, 4):
        src = (Y + j) % 4
        arrived(gr2.at[src], s["q_y"], src)
    g2[...] = (gr2[0] + gr2[1]) + (gr2[2] + gr2[3])
    for k in range(1, 4):
        send(g2.at[(zl + k) % 4], gr3.at[zl], s["q_z"], zl, dev(X, Y, zpeer(k), C))
    for b in range(16, 32):
        finish(b)
    gr3[zl] = g2[zl]
    for j in range(1, 4):
        src = (zl + j) % 4
        arrived(gr3.at[src], s["q_z"], src)
    g3[...] = (gr3[0] + gr3[1]) + (gr3[2] + gr3[3])
    for k in (1, 3, 2):
        send(g3, gr4.at[X], s["q_x"], X, dev(X + k, Y, Z, C))
    gr4[X] = g3[...]

    for j in range(1, 4):
        src = (Y + j) % 4
        arrived(dlv.at[src], s["r_d"], src)

    @pl.when(X != Y)
    def _():
        arrived(dlv.at[Y], s["r_d"], Y)

    out_w[...] = dlv[...].reshape(128, 512)

    for j in range(1, 4):
        src = (X + j) % 4
        arrived(gr4.at[src], s["q_x"], src)
    result = (gr4[0] + gr4[1]) + (gr4[2] + gr4[3])
    out_g[...] = jnp.sum(result, axis=0, keepdims=True) * average

    for copy in started:
        copy.wait_send()

    @pl.when(X != Y)
    def _():
        to_diagonal().wait_send()


def scratch():
    def sem(*shape):
        return pltpu.SemaphoreType.DMA(shape)

    vmem = pltpu.VMEM
    return dict(
        wbuf=vmem((2, 8, 4, 2, 64, 512), BF16),
        vgx=vmem((8, 256, 512), BF16),
        vga=vmem((2, 256, 512), BF16),
        hid=vmem((32, 256, 128), BF16),
        hx=vmem((4, 8, 256, 128), BF16),
        gainb=vmem((2, 4, 4, 8, 128), F32),
        invt=vmem((8, 256), F32),
        invx=vmem((8, 8, 256), F32),
        invb=vmem((256, 128), F32),
        invc=vmem((8, 256, 128), F32),
        normed=vmem((8, 256, 128), BF16),
        part=vmem((4, 4, 32, 512), F32),
        yrecv=vmem((4, 4, 32, 512), F32),
        ysum=vmem((4, 32, 512), F32),
        zrecv=vmem((4, 32, 512), F32),
        fin=vmem((32, 512), F32),
        dlv=vmem((4, 32, 512), F32),
        gs=vmem((32, 256, 128), F32),
        center=vmem((256, 128), F32),
        gg=vmem((2, 4, 4, 8, 128), F32),
        g1=vmem((4, 4, 8, 128), F32),
        gr1=vmem((4, 4, 8, 128), F32),
        gr2=vmem((4, 4, 8, 128), F32),
        g2=vmem((4, 8, 128), F32),
        gr3=vmem((4, 8, 128), F32),
        g3=vmem((8, 128), F32),
        gr4=vmem((4, 8, 128), F32),
        l_w=pltpu.SemaphoreType.DMA,
        l_vg=pltpu.SemaphoreType.DMA((2,)),
        l_h=pltpu.SemaphoreType.DMA((32,)),
        l_o=pltpu.SemaphoreType.DMA((4,)),
        a_y=sem(4),
        a_p=sem(5),
        a_m=sem(5),
        b_p=sem(5),
        b_m=sem(5),
        b_y=sem(8, 4),
        d_a=sem(8),
        d_b=sem(8),
        g_y=sem(4),
        g_z=sem(4),
        g_c=sem(1),
        vg_x=sem(4),
        vg_c=sem(4),
        vg_t=sem(1),
        h_x=sem(4, 8),
        i_x=sem(8),
        r_y=sem(4, 4),
        r_z=sem(4),
        r_d=sem(4),
        r_s=pltpu.SemaphoreType.DMA,
        sent=sem(176),
        q_c=sem(1),
        q_y=sem(4),
        q_z=sem(4),
        q_x=sem(4),
    )


def local(hidden, norm_gain, value_weight, value_grad):
    any_space = pl.BlockSpec(memory_space=pl.ANY)
    in_vmem = pl.BlockSpec(memory_space=pltpu.VMEM)
    names = scratch()
    input_grad, weight_grad, gain_grad = pl.pallas_call(
        lambda *refs: kernel(*refs[:7], dict(zip(names, refs[7:]))),
        out_shape=(
            jax.ShapeDtypeStruct((256, D), BF16),
            jax.ShapeDtypeStruct((128, 512), F32),
            jax.ShapeDtypeStruct((1, 128), F32),
        ),
        in_specs=[any_space, in_vmem, any_space, any_space],
        out_specs=(in_vmem, in_vmem, in_vmem),
        scratch_shapes=list(names.values()),
        compiler_params=pltpu.CompilerParams(
            collective_id=0, has_side_effects=True, vmem_limit_bytes=48 * 2**20
        ),
        name="rmsnorm_value_backward",
    )(hidden, norm_gain.reshape(1, 128), value_weight.reshape(2, 64, 512), value_grad)
    return (input_grad, weight_grad, gain_grad.reshape(128))


def solution(mesh):
    return jax.shard_map(
        local,
        mesh=mesh,
        in_specs=(P(("rep", "fsdp"), None), P("fsdp"), P("fsdp", "tp"), P(("rep", "fsdp"), "tp")),
        out_specs=(P(("rep", "fsdp"), None), P("fsdp", "tp"), P("fsdp")),
        check_vma=False,
    )
```

time: 475 us -> 95 us (0.20)
  waiting for transfers between devices: 268 us -> 0 us
  blocking collectives: 163 us -> 0 us
  Pallas kernels: 0 us -> 87.2 us
  other arithmetic: 17.6 us -> 0 us
  between operations: 14.4 us -> 0.65 us
  matrix products: 10 us -> 0 us
  local copies, waits for them, and re-layouts: 1.85 us -> 6.63 us
    all_gather x3 -> x0, waiting for transfers between devices: 255 us -> none  [the longest x2 189 us: gathered_total(): return lax.all_gather(array, axis).sum(0)]
    unnamed x1 -> x0, blocking collectives: 118 us -> none
    pallas_call x0 -> x1, Pallas kernels: none -> 87.2 us  [local(): pl.pallas_call(lambda *refs: kernel(*refs[:7], dict(zip(names, refs[7:]))...]
    all_gather x2 -> x0, blocking collectives: 44.4 us -> none  [the longest x1 34.4 us: local(): full_gain = lax.all_gather(norm_gain, 'fsdp', axis=0, tiled=True)]
    reduce_sum x5 -> x0, other arithmetic: 11.6 us -> none  [the longest x3 7.71 us: gathered_total(): return lax.all_gather(array, axis).sum(0)]
    reduce_scatter x1 -> x0, waiting for transfers between devices: 11.6 us -> none  [local(): lax.psum_scatter(weight_term(value_weight.shape[0] * lax.axis_size('fsdp'...]
    dot_general x2 -> x0, matrix products: 10 us -> none  [the longest x1 5.4 us: project(): jnp.dot(value_grad, weight_piece.T, preferred_element_type=jnp.float32)]
    unnamed x10 -> x11, local copies, waits for them, and re-layouts: 1.85 us -> 6.63 us
  transfers between devices with their start and end apart: 4 -> 0, of which waited for: 4 -> 0; matrix products, arithmetic and copies ran while one was open for 4% -> 0% of each run, Pallas kernels for 0% -> 0%
where the time goes in v1:
time: 95 us; the launch traced here: 94.5 us
  Pallas kernels  87.2 us (92%)
  local copies, waits for them, and re-layouts  6.63 us (7%)
    pallas_call x1, Pallas kernels, local(): pl.pallas_call(lambda *refs: kernel(*refs[:7], dict(zip(names, refs[7:]))...  87.2 us
    unnamed x11, local copies, waits for them, and re-layouts  6.63 us

profile of v1, /device:TPU:24, one launch (start us, length us, event | category | flops | bytes accessed | tf_op | source)
XLA Modules:
  0.0 94.5 jit_solution(90638118907935008)
XLA Ops:
  0.6 0.0 copy-start
  0.6 1.6 %copy-done = bf16[256,4096]{1,0:T(8,128)(2,1)S(1)} copy-done((bf16[256,4096]{1,0:T(8,128)(2,1)S(1)}, bf16[256,4096]{1,0:T(8,128)(2,1)}, u32[]{:S(2)}) %copy-start) | copy-done | bytes 2097176
  2.2 0.0 copy-start.1
  2.2 0.9 %copy-done.1 = bf16[256,512]{1,0:T(8,128)(2,1)S(1)} copy-done((bf16[256,512]{1,0:T(8,128)(2,1)S(1)}, bf16[256,512]{1,0:T(8,128)(2,1)}, u32[]{:S(2)}) %copy-start.1) | copy-done | bytes 262168
  3.2 0.0 copy-start.2
  3.2 0.9 copy-done.2
  4.1 0.0 copy-start.3
  4.1 0.7 copy-done.3
  4.7 87.2 %rmsnorm_value_backward.1 = (bf16[256,4096]{1,0:T(8,128)(2,1)S(1)}, f32[128,512]{1,0:T(8,128)S(1)}, f32[1,128]{1,0:T(1,128)S(1)}) custom-call(bf16[256,4096]{1,0:T(8,128)(2,1)S(1)} %copy-done, f32[1,128]{1,0:T(1,128)S(1)} %bitcast.4, bf16[2,64,512]{2,1,0:T(8,128)(2,1)S(1)} %bitcast.3, bf16[256,512]{1,0:T(8,128)(2,1)S(1)} %copy-done.1), custom_call_target="tpu_custom_call" | custom-call | tf_op jit(solution)/shard_map/rmsnorm_value_backward/pallas_call | solution.py:473
  92.0 1.3 %copy.10 = bf16[256,4096]{1,0:T(8,128)(2,1)} copy(bf16[256,4096]{1,0:T(8,128)(2,1)S(1)} %get-tuple-element.12) | data formatting | bytes 4194304
  93.3 0.7 copy.11
  94.0 0.5 copy.12
Async XLA Ops:
  0.6 1.6 %copy-start = (bf16[256,4096]{1,0:T(8,128)(2,1)S(1)}, bf16[256,4096]{1,0:T(8,128)(2,1)}, u32[]{:S(2)}) copy-start(bf16[256,4096]{1,0:T(8,128)(2,1)} %refs_0_.1) | copy-start | bytes 6291460
  2.2 0.9 %copy-start.1 = (bf16[256,512]{1,0:T(8,128)(2,1)S(1)}, bf16[256,512]{1,0:T(8,128)(2,1)}, u32[]{:S(2)}) copy-start(bf16[256,512]{1,0:T(8,128)(2,1)} %refs_3_.1) | copy-start | bytes 786436
  3.2 0.9 copy-start.2
  4.1 0.7 copy-start.3
